TPU v7x, 256 devices: a whole 4x4x8 slice. The times are simulated.
256 devices in a mesh: gx: 4 (over x), gy: 8 (over z_hi, y), gz: 8 (over z_lo, core).
Axes of the slice: x: 4, y: 4, z: 8 (z_hi: 2, z_lo: 4; z = z_hi * 4 + z_lo), core: 2. Of those that a mesh axis runs over, the one named last changes fastest.
Arguments:
- velocity: float32 [3, 128, 768, 2048], P(None, 'gx', 'gy', 'gz'), may hold values from -6 to 6
Outputs:
- magnitude: float32 [128, 768, 2048], P('gx', ('gy', 'gz'))
- level_one: float32 [64, 384, 1024], P('gx', 'gy')
- level_two: float32 [32, 192, 512], P('gx', 'gy')
- level_three: float32 [16, 96, 256], P('gx', 'gy')
- level_four: float32 [8, 48, 128], P('gx', 'gy')
- level_five: float32 [4, 24, 64], P('gx', 'gy')
All inputs are finite; a program needn't handle non-finite values.
Results may differ from a plain program's by a relative error of at most 0.000075.
Values sent between devices are 32-bit elements; how exact they have to be, the bound alone decides.
A program may use at most 256 MiB of HBM per device.

v0:
```python
import jax
import jax.numpy as jnp
from jax import lax
from jax.sharding import PartitionSpec as P


def extended(value, sides, width):
    for axis, dim in sides:
        peers, length = (lax.axis_size(axis), value.shape[dim])
        up = [(i, (i + 1) % peers) for i in range(peers)]
        down = [(j, i) for i, j in up]
        last = lax.slice_in_dim(value, length - width, length, axis=dim)
        leading = lax.slice_in_dim(value, 0, width, axis=dim)
        before = lax.ppermute(last, axis, up)
        after = lax.ppermute(leading, axis, down)
        value = jnp.concatenate([before, value, after], axis=dim)
    return value


def depth_diff(field, before, after):
    ahead = jnp.roll(field, -1, 2)
    behind = jnp.roll(field, 1, 2)
    depth_index = lax.broadcasted_iota(jnp.int32, field.shape, 2)
    ahead = jnp.where(depth_index == field.shape[2] - 1, after[:, :, None], ahead)
    behind = jnp.where(depth_index == 0, before[:, :, None], behind)
    return (ahead - behind) * 0.5


def vorticity(padded, before, after):
    inner = padded[:, 1:-1, 1:-1, :]

    def first_diff(comp):
        return (padded[comp, 2:, 1:-1, :] - padded[comp, :-2, 1:-1, :]) * 0.5

    def second_diff(comp):
        return (padded[comp, 1:-1, 2:, :] - padded[comp, 1:-1, :-2, :]) * 0.5

    def third_diff(comp):
        return depth_diff(inner[comp], before[comp], after[comp])

    curl_first = second_diff(2) - third_diff(1)
    curl_second = third_diff(0) - first_diff(2)
    curl_third = first_diff(1) - second_diff(0)
    return jnp.sqrt(
        1.0 + curl_first * curl_first + curl_second * curl_second + curl_third * curl_third
    )


def pooled(field):
    rows, cols, depth = field.shape
    summed = field.reshape(rows // 2, 2, cols, depth).sum(axis=1)
    summed = summed.reshape(rows // 2, cols // 2, 2, depth).sum(axis=2)
    pairing = (
        lax.broadcasted_iota(jnp.int32, (depth, depth // 2), 0) // 2
        == lax.broadcasted_iota(jnp.int32, (depth, depth // 2), 1)
    ).astype(jnp.float32)
    merged = jnp.dot(
        summed.reshape(-1, depth),
        pairing,
        precision=lax.Precision.HIGHEST,
        preferred_element_type=jnp.float32,
    )
    return merged.reshape(rows // 2, cols // 2, depth // 2) * 0.125


def end_planes(velocity):
    return jnp.concatenate([velocity[..., :1], velocity[..., -1:]], axis=3)


def on_device(velocity):
    padded = extended(velocity, (("gx", 1), ("gy", 2)), 1)
    planes = extended(end_planes(velocity), (("gz", 3),), 1)
    block_mag = vorticity(padded, planes[..., 0], planes[..., 3])
    pencil = lax.all_to_all(block_mag, "gz", split_axis=1, concat_axis=2, tiled=True)
    level_one = lax.all_gather(pooled(pencil), "gz", axis=1, tiled=True)
    level_two = pooled(level_one)
    level_three = pooled(level_two)
    level_four = pooled(level_three)
    level_five = pooled(level_four)
    return (pencil, level_one, level_two, level_three, level_four, level_five)


def solution(mesh):
    in_specs = (P(None, "gx", "gy", "gz"),)
    out_specs = (
        P("gx", ("gy", "gz"), None),
        P("gx", "gy", None),
        P("gx", "gy", None),
        P("gx", "gy", None),
        P("gx", "gy", None),
        P("gx", "gy", None),
    )
    return jax.shard_map(
        on_device, mesh=mesh, in_specs=in_specs, out_specs=out_specs, check_vma=False
    )
```

profile of v0, /device:TPU:2, one launch (start us, length us, event | category | flops | bytes accessed | tf_op | source)
XLA Modules:
  0.0 282.3 jit_solution(7499738922202959206)
XLA Ops:
  7.2 1.1 fusion.68
  8.3 1.0 copy.115
  9.3 2.2 collective-permute-start.1
  11.5 1.0 copy.114
  12.6 0.0 collective-permute-start
  12.6 8.7 %fusion.67 = (f32[3,32,96,1]{3,2,1,0:T(8,128)}, f32[3,32,96,1]{3,2,1,0:T(8,128)}) fusion(f32[3,32,96,256]{3,2,1,0:T(8,128)} %param.1), kind=kLoop, calls=%fused_computation.116 | loop fusion | bytes 147456 | tf_op jit(solution)/shard_map/slice | solution.py:67
  21.2 3.1 %copy.140 = f32[3,32,96,1]{2,1,3,0:T(8,128)S(1)} copy(f32[3,32,96,1]{3,2,1,0:T(8,128)} %get-tuple-element.51) | data formatting | bytes 73728
  24.3 0.1 collective-permute-start.5
  24.4 3.1 %copy.139 = f32[3,32,96,1]{2,1,3,0:T(8,128)S(1)} copy(f32[3,32,96,1]{3,2,1,0:T(8,128)} %get-tuple-element.50) | data formatting | bytes 73728
  27.5 3.8 %collective-permute-start.4 = (f32[3,32,96,1]{2,1,3,0:T(8,128)S(1)}, f32[3,32,96,1]{2,1,3,0:T(8,128)}, u32[]{:S(2)}, u32[]{:S(2)}) collective-permute-start(f32[3,32,96,1]{2,1,3,0:T(8,128)S(1)} %copy.139), channel_id=1, source_target_pairs={{1,0},{2,1},{3,2},{4,3},{5,4},{6,5},{7,6},{0,7},{9,8},{10,9},{11,1... | collective-permute-start | bytes 110600 | tf_op jit(solution)/shard_map/ppermute | solution.py:15
  31.3 15.9 %constant_dynamic-update-slice_fusion = (f32[3,33,96,256]{3,1,2,0:T(8,128)}, f32[3,32,96,256]{3,1,2,0:T(8,128)}) fusion(f32[3,32,96,256]{3,2,1,0:T(8,128)} %param.1), kind=kLoop, calls=%fused_computation.100 | loop fusion | bytes 28311552
  47.2 3.6 %slice_bitcast_fusion = (f32[32,96,256]{2,0,1:T(8,128)S(1)}, f32[32,96,256]{2,0,1:T(8,128)S(1)}) fusion(f32[3,32,96,256]{3,1,2,0:T(8,128)} %get-tuple-element.55), kind=kLoop, calls=%fused_computation.28 | loop fusion | bytes 12582912 | tf_op jit(solution)/shard_map/squeeze | solution.py:39
  50.8 3.6 %fusion.69 = (f32[32,96,1]{2,0,1:T(8,128)}, f32[32,96,1]{2,0,1:T(8,128)}, f32[32,96,1]{2,0,1:T(8,128)}, f32[32,96,1]{2,0,1:T(8,128)}) fusion(f32[32,96,256]{2,0,1:T(8,128)S(1)} %get-tuple-element.52, f32[32,96,256]{2,0,1:T(8,128)S(1)} %get-tuple-element.53), kind=kLoop, calls=%fused_computation.118 | loop fusion | bytes 98304 | tf_op jit(solution)/shard_map/jit(_roll_static)/slice | solution.py:22
  54.3 6.5 %fusion.70 = (f32[32,96,255]{2,0,1:T(8,128)}, f32[32,96,255]{2,0,1:T(8,128)}, f32[32,96,255]{2,0,1:T(8,128)}, f32[32,96,255]{2,0,1:T(8,128)}) fusion(f32[32,96,256]{2,0,1:T(8,128)S(1)} %get-tuple-element.52, f32[32,96,256]{2,0,1:T(8,128)S(1)} %get-tuple-element.53), kind=kLoop, calls=%fused_computation.119 | loop fusion | bytes 25067520 | tf_op jit(solution)/shard_map/jit(_roll_static)/slice | solution.py:22
  60.8 0.5 iota_compare_fusion.6
  61.3 0.0 collective-permute-done.5
  61.3 0.7 slice_bitcast_fusion.4
  62.1 0.0 copy-start
  62.1 0.0 collective-permute-done.1
  62.1 0.0 collective-permute-done
  62.1 1.8 pad_maximum_fusion.9
  63.9 9.4 %collective-permute-start.2 = (f32[3,34,1,256]{3,1,2,0:T(8,128)}, f32[3,34,1,256]{3,1,2,0:T(8,128)}, u32[]{:S(2)}, u32[]{:S(2)}) collective-permute-start(f32[3,34,1,256]{3,1,2,0:T(8,128)} %get-tuple-element.48), channel_id=1, source_target_pairs={{8,0},{16,8},{24,16},{32,24},{40,32},{48,40},{56,48},{0,56},{9,1},... | collective-permute-start | bytes 313352 | tf_op jit(solution)/shard_map/ppermute | solution.py:15
  73.3 0.0 collective-permute-start.3
  73.3 0.0 collective-permute-done.4
  73.3 1.3 slice_bitcast_fusion.5
  74.7 0.1 copy.121
  74.8 0.1 copy.124
  74.9 1.4 copy.118
  76.3 1.4 copy.122
  77.7 7.8 %dynamic-update-slice.1 = f32[3,33,96,256]{3,1,2,0:T(8,128)} dynamic-update-slice(f32[3,33,96,256]{3,1,2,0:T(8,128)} %get-tuple-element.54, f32[3,1,96,256]{3,1,2,0:T(1,128)S(1)} %collective-permute-done.1, s32[]{} %constant.86, s32[]{} %constant.87, s32[]{} %constant.86, s32[]{} %constant.86) | dynamic-update-slice | bytes 589828 | tf_op jit(solution)/shard_map/concatenate | solution.py:16
  85.5 0.0 collective-permute-done.2
  85.5 0.0 collective-permute-done.3
  85.6 0.0 copy-done
  85.6 21.7 %fusion.12 = f32[32,96,256]{2,0,1:T(8,128)} fusion(f32[3,34,1,256]{3,1,2,0:T(8,128)} %collective-permute-done.3, f32[3,1,96,256]{3,1,2,0:T(1,128)S(1)} %collective-permute-done.1, f32[3,32,96,256]{3,1,2,0:T(8,128)} %get-tuple-element.55, f32[3,1,96,256]{3,1,2,0:T(1,128)} %collective-permute-done, f32[3,34,1,256]{3,1,2,0:T(8,128)} %collective-permute-done.2, ...), kind=kLoop, calls=%fused_computation.13 | loop fusion | flops 33816576 | bytes 32305664 | tf_op jit(solution)/shard_map/sqrt | solution.py:44
  107.3 3.7 %all-to-all-start = ((f32[32,96,256]{2,0,1:T(8,128)}), f32[32,96,256]{2,0,1:T(8,128)S(1)}, u32[]{:S(2)}, u32[]{:S(2)}) async-start(f32[32,96,256]{2,0,1:T(8,128)} %fusion.12), calls=%async_computation | async-start | bytes 6291456 | tf_op jit(solution)/shard_map/all_to_all | solution.py:74
  111.0 0.3 all-gather.2.cloned.1.call-start
  111.3 71.1 %all-to-all-done = f32[32,96,256]{2,0,1:T(8,128)S(1)} async-done(((f32[32,96,256]{2,0,1:T(8,128)}), f32[32,96,256]{2,0,1:T(8,128)S(1)}, u32[]{:S(2)}, u32[]{:S(2)}) %all-to-all-start) | async-done | bytes 3145760 | tf_op jit(solution)/shard_map/all_to_all | solution.py:74
  182.4 3.9 %copy.127 = f32[32,12,8,256]{3,2,0,1:T(8,128)} copy(f32[32,12,8,256]{3,0,1,2:T(8,128)S(1)} %bitcast.83) | data formatting | bytes 6291456 | tf_op jit(solution)/shard_map/all_to_all | solution.py:74
  186.3 5.2 %reshape.90 = f32[16,2,12,2048]{3,1,0,2:T(2,128)} reshape(f32[32,12,8,256]{3,2,0,1:T(8,128)} %copy.127) | data formatting | bytes 6291456 | tf_op jit(solution)/shard_map/reshape | solution.py:51
  191.4 7.0 %reduce_sum.90 = f32[16,12,2048]{2,0,1:T(8,128)} reduce(f32[16,2,12,2048]{3,1,0,2:T(2,128)} %reshape.90, f32[]{:T(128)} %constant.81.clone.1), dimensions={1}, to_apply=%region_0.1 | reduce | flops 393216 | bytes 4718596 | tf_op jit(solution)/shard_map/reduce_sum | solution.py:51
  198.4 2.5 reduce_sum.91
  200.8 5.2 %fusion.35 = f32[16,6,1024]{2,0,1:T(8,128)} fusion(f32[16,6,2048]{2,0,1:T(8,128)} %reduce_sum.91, s32[2048]{0:T(1024)S(1)} %get-tuple-element.82, s32[2048]{0:T(1024)S(1)} %get-tuple-element.83, pred[2048]{0:T(1024)(128)(4,1)S(1)} %fusion.60), kind=kOutput, calls=%fused_computation.48 | convolution fusion | flops 2420211712 | bytes 1198080 | tf_op jit(solution)/shard_map/dot_general | solution.py:57
  206.0 0.0 all-gather.2.cloned.1.call-update
  206.1 2.1 copy.141
  208.2 44.7 %all-gather.2.cloned.1.call-done = f32[16,48,1024]{2,0,1:T(8,128)} async-done(((f32[16,6,1024]{2,0,1:T(8,128)}), f32[16,48,1024]{2,0,1:T(8,128)}) %all-gather.2.cloned.1.call-update) | async-done | bytes 3145744 | tf_op jit(solution)/shard_map/all_gather | solution.py:75
  253.0 4.0 %reshape.92 = f32[8,2,48,1024]{3,1,0,2:T(2,128)S(1)} reshape(f32[16,48,1024]{2,0,1:T(8,128)} %all-gather.2.cloned.1.call-done) | data formatting | bytes 6291456 | tf_op jit(solution)/shard_map/reshape | solution.py:51
  256.9 5.4 %reduce_sum.92 = f32[8,48,1024]{2,0,1:T(8,128)} reduce(f32[8,2,48,1024]{3,1,0,2:T(2,128)S(1)} %reshape.92, f32[]{:T(128)} %constant.81.clone.1), dimensions={1}, to_apply=%region_2.3 | reduce | flops 393216 | bytes 4718596 | tf_op jit(solution)/shard_map/reduce_sum | solution.py:51
  262.4 0.0 copy-start.1
  262.4 2.6 reduce_sum.93
  265.0 3.3 %bitcast_reduce_fusion = (f32[4,24,512]{2,1,0:T(8,128)S(1)}, f32[8,24,512]{2,1,0:T(8,128)}) fusion(s32[1024]{0:T(1024)S(1)} %get-tuple-element.84, s32[1024]{0:T(1024)S(1)} %get-tuple-element.85, pred[1024]{0:T(1024)(128)(4,1)S(1)} %fusion.63, f32[8,24,1024]{2,0,1:T(8,128)} %reduce_sum.93), kind=kOutput, calls=%fused_computation.59 | convolution fusion | flops 1209155584 | bytes 1385472 | tf_op jit(solution)/shard_map/dot_general | solution.py:57
  268.3 0.1 copy.138
  268.4 0.1 reduce_sum.95
  268.5 0.5 bitcast_reduce_fusion.1
  269.0 0.3 fusion.73
  269.4 0.2 fusion.38
  269.6 0.6 copy.137
  270.2 0.6 copy.136
  270.8 0.7 copy.135
  271.5 0.0 copy-done.1
  271.5 3.5 %copy.134 = f32[16,48,1024]{2,1,0:T(8,128)} copy(f32[16,48,1024]{2,0,1:T(8,128)S(1)} %copy-done.1) | data formatting | bytes 6291456
  (14 shorter events, 0.1 us)
Async XLA Ops:
  9.3 52.8 %collective-permute-start.1 = (f32[3,1,96,256]{3,1,2,0:T(1,128)}, f32[3,1,96,256]{3,1,2,0:T(1,128)S(1)}, u32[]{:S(2)}, u32[]{:S(2)}) collective-permute-start(f32[3,1,96,256]{3,1,2,0:T(1,128)} %copy.115), channel_id=1, source_target_pairs={{64,0},{128,64},{192,128},{0,192},{65,1},{129,65},{193,129},{1,193... | collective-permute-start | bytes 884744 | tf_op jit(solution)/shard_map/ppermute | solution.py:15
  12.6 49.5 %collective-permute-start = (f32[3,1,96,256]{3,1,2,0:T(1,128)}, f32[3,1,96,256]{3,1,2,0:T(1,128)}, u32[]{:S(2)}, u32[]{:S(2)}) collective-permute-start(f32[3,1,96,256]{3,1,2,0:T(1,128)} %copy.114), channel_id=1, source_target_pairs={{0,64},{64,128},{128,192},{192,0},{1,65},{65,129},{129,193},{193,1... | collective-permute-start | bytes 884744 | tf_op jit(solution)/shard_map/ppermute | solution.py:14
  24.3 37.0 %collective-permute-start.5 = (f32[3,32,96,1]{2,1,3,0:T(8,128)S(1)}, f32[3,32,96,1]{2,1,3,0:T(8,128)}, u32[]{:S(2)}, u32[]{:S(2)}) collective-permute-start(f32[3,32,96,1]{2,1,3,0:T(8,128)S(1)} %copy.140), channel_id=1, source_target_pairs={{0,1},{1,2},{2,3},{3,4},{4,5},{5,6},{6,7},{7,0},{8,9},{9,10},{10,1... | collective-permute-start | bytes 110600 | tf_op jit(solution)/shard_map/ppermute | solution.py:14
  27.5 45.8 %collective-permute-start.4 = (f32[3,32,96,1]{2,1,3,0:T(8,128)S(1)}, f32[3,32,96,1]{2,1,3,0:T(8,128)}, u32[]{:S(2)}, u32[]{:S(2)}) collective-permute-start(f32[3,32,96,1]{2,1,3,0:T(8,128)S(1)} %copy.139), channel_id=1, source_target_pairs={{1,0},{2,1},{3,2},{4,3},{5,4},{6,5},{7,6},{0,7},{9,8},{10,9},{11,1... | collective-permute-start | bytes 110600 | tf_op jit(solution)/shard_map/ppermute | solution.py:15
  62.1 23.5 %copy-start = (f32[32,96,255]{2,0,1:T(8,128)S(1)}, f32[32,96,255]{2,0,1:T(8,128)}, u32[]{:S(2)}) copy-start(f32[32,96,255]{2,0,1:T(8,128)} %get-tuple-element.60) | copy-start | bytes 9400324
  63.9 21.6 %collective-permute-start.2 = (f32[3,34,1,256]{3,1,2,0:T(8,128)}, f32[3,34,1,256]{3,1,2,0:T(8,128)}, u32[]{:S(2)}, u32[]{:S(2)}) collective-permute-start(f32[3,34,1,256]{3,1,2,0:T(8,128)} %get-tuple-element.48), channel_id=1, source_target_pairs={{8,0},{16,8},{24,16},{32,24},{40,32},{48,40},{56,48},{0,56},{9,1},... | collective-permute-start | bytes 313352 | tf_op jit(solution)/shard_map/ppermute | solution.py:15
  73.3 12.2 %collective-permute-start.3 = (f32[3,34,1,256]{3,1,2,0:T(8,128)}, f32[3,34,1,256]{3,1,2,0:T(8,128)}, u32[]{:S(2)}, u32[]{:S(2)}) collective-permute-start(f32[3,34,1,256]{3,1,2,0:T(8,128)} %get-tuple-element.49), channel_id=1, source_target_pairs={{0,8},{8,16},{16,24},{24,32},{32,40},{40,48},{48,56},{56,0},{1,9},... | collective-permute-start | bytes 313352 | tf_op jit(solution)/shard_map/ppermute | solution.py:14
  107.3 75.1 %all-to-all-start = ((f32[32,96,256]{2,0,1:T(8,128)}), f32[32,96,256]{2,0,1:T(8,128)S(1)}, u32[]{:S(2)}, u32[]{:S(2)}) async-start(f32[32,96,256]{2,0,1:T(8,128)} %fusion.12), calls=%async_computation | async-start | bytes 6291456 | tf_op jit(solution)/shard_map/all_to_all | solution.py:74
  111.0 142.0 %all-gather.2.cloned.1.call-start = ((), (), s32[]{:S(2)}) async-start(), calls=%async_computation.1 | async-start | bytes 3538944 | tf_op jit(solution)/shard_map/all_gather | solution.py:75
  262.4 9.1 %copy-start.1 = (f32[16,48,1024]{2,0,1:T(8,128)S(1)}, f32[16,48,1024]{2,0,1:T(8,128)}, u32[]{:S(2)}) copy-start(f32[16,48,1024]{2,0,1:T(8,128)} %all-gather.2.cloned.1.call-done) | copy-start | bytes 9437188
Sparse Core Ops, SparseCore 0:
  206.1 46.7 all-gather.1
where the time goes:
time: 288 us; the launch traced here: 282 us
  waiting for transfers between devices  116 us (40%)
  local copies, waits for them, and re-layouts  81.1 us (28%)
  other arithmetic  41.7 us (14%)
  starting transfers between devices  19.4 us (7%)
  between operations  14.6 us (5%)
  matrix products  9.52 us (3%)
    all_to_all x1, waiting for transfers between devices, on_device(): lax.all_to_all(block_mag, 'gz', split_axis=1, concat_axis=2, tiled=True)  71.1 us
    all_gather x1, waiting for transfers between devices, on_device(): level_one = lax.all_gather(pooled(pencil), 'gz', axis=1, tiled=True)  44.7 us
    unnamed x11, local copies, waits for them, and re-layouts  27.4 us
    sqrt x1, other arithmetic, vorticity(): jnp.sqrt(1.0 + curl_first * curl_first + curl_second * curl_second + curl...  21.7 us
    ppermute x3, starting transfers between devices, extended(): after = lax.ppermute(leading, axis, down)  15.4 us
    reduce_sum x2, other arithmetic, pooled(): summed = field.reshape(rows // 2, 2, cols, depth).sum(axis=1)  12.4 us
    slice x2, local copies, waits for them, and re-layouts, depth_diff(): behind = jnp.roll(field, 1, 2)  10.1 us
    dot_general x5, matrix products, pooled(): jnp.dot(summed.reshape(-1, depth), pairing, precision=lax.Precision.HIGHE...  9.52 us
  transfers between devices with their start and end apart: 8, of which 2 were waited for; matrix products, arithmetic and copies ran while one was open for 22% of the time, Pallas kernels for 0%

commit v1 on v0

v1 whole, which is shorter than its diff:
```python
import functools

import jax
import jax.numpy as jnp
from jax import lax
from jax.experimental import pallas as pl
from jax.experimental.pallas import tpu as pltpu
from jax.sharding import PartitionSpec as P

F32 = jnp.float32
GROUP = 8
CHIPS = 4
ORDER = (1, 2, 0, 3)
U, V, W = (0, 1, 2)


def pairing():
    upper = lax.broadcasted_iota(jnp.int32, (256, 128), 0) // 2
    lower = lax.broadcasted_iota(jnp.int32, (256, 128), 1)
    return (upper == lower).astype(F32)


def lane_pairs(value, pair):
    return jnp.dot(value, pair, precision=lax.Precision.HIGHEST, preferred_element_type=F32)


def flip(index, mask):
    bits = [(index // w) % 2 for w in (1, 2, 4)]
    bits = [1 - b if (mask >> i) % 2 else b for i, b in enumerate(bits)]
    return bits[0] + 2 * bits[1] + 4 * bits[2]


def exchange(
    vel_hbm, pencil, level, vel, planes, block, own, halves, edge_out, edge_in, row_out, row_in,
    load_sem, x_sem, y_sem, z_sem, a2a_send, a2a_recv, level_send, level_recv, own_sem, peer_sem,
):
    gx, gy, gz = (lax.axis_index("gx"), lax.axis_index("gy"), lax.axis_index("gz"))
    chip, core = (gz // 2, gz % 2)
    x_sides = [{"gx": (gx + 3) % 4}, {"gx": (gx + 1) % 4}]
    y_sides = [{"gy": (gy + 7) % 8}, {"gy": (gy + 1) % 8}]
    z_sides = [{"gz": (gz + 7) % 8}, {"gz": (gz + 1) % 8}]

    loads = [
        pltpu.make_async_copy(vel_hbm.at[c], vel.at[c, 1:33], load_sem.at[c]) for c in (U, V, W)
    ]
    for copy in loads:
        copy.start()

    barrier = pltpu.get_barrier_semaphore()
    for mask in range(1, 8):
        pl.semaphore_signal(barrier, inc=1, device_id={"gz": flip(gz, mask)})
    for side in x_sides + y_sides:
        pl.semaphore_signal(barrier, inc=1, device_id=side)

    row = lax.broadcasted_iota(jnp.int32, (96, 128), 0)
    lane = lax.broadcasted_iota(jnp.int32, (96, 128), 1)

    loads[U].wait()
    loads[V].wait()

    def pack_edges(x, carry):
        first, last = carry
        for comp in (U, V):
            at = comp * 32 + x
            first = jnp.where(lane == at, pltpu.roll(vel[comp, x + 1, :, 0:128], at, 1), first)
            last = jnp.where(lane == at, pltpu.roll(vel[comp, x + 1, :, 128:256], at + 1, 1), last)
        return first, last

    zero = jnp.zeros((96, 128), F32)
    first, last = lax.fori_loop(0, 32, pack_edges, (zero, zero))
    edge_out[0] = first
    edge_out[1] = last
    loads[W].wait()

    def pack_rows(x, carry):
        for spot, comp in enumerate((U, W)):
            for half in (0, 1):
                lanes = slice(half * 128, half * 128 + 128)
                row_out[0, spot, x, half : half + 1, :] = vel[comp, x + 1, 0:1, lanes]
                row_out[1, spot, x, half : half + 1, :] = vel[comp, x + 1, 95:96, lanes]
        return carry

    lax.fori_loop(0, 32, pack_rows, 0)
    pl.semaphore_wait(barrier, 11)

    halos = []
    for side in (0, 1):
        halos.append(
            pltpu.make_async_remote_copy(
                edge_out.at[side], edge_in.at[1 - side], z_sem.at[0, side], z_sem.at[1, 1 - side],
                device_id=z_sides[side],
            )
        )
        halos.append(
            pltpu.make_async_remote_copy(
                row_out.at[side], row_in.at[1 - side], y_sem.at[0, side], y_sem.at[1, 1 - side],
                device_id=y_sides[side],
            )
        )
        halos.append(
            pltpu.make_async_remote_copy(
                vel.at[1:3, 32 * side - side + 1], vel.at[1:3, 33 - 33 * side],
                x_sem.at[0, side], x_sem.at[1, 1 - side], device_id=x_sides[side],
            )
        )
    for copy in halos:
        copy.start()
    for copy in (halos[0], halos[3], halos[1], halos[4]):
        copy.wait_recv()

    pair = pairing()

    def second_diff(comp, spot, x, half):
        lanes = slice(half * 128, half * 128 + 128)
        value = vel[comp, x + 1, :, lanes]
        before = row_in[0, spot, x, half : half + 1, :]
        after = row_in[1, spot, x, half : half + 1, :]
        ahead = jnp.where(row == 95, after, pltpu.roll(value, 95, 0))
        behind = jnp.where(row == 0, before, pltpu.roll(value, 1, 0))
        return ahead - behind

    def third_diff(comp, x, half):
        low = vel[comp, x + 1, :, 0:128]
        high = vel[comp, x + 1, :, 128:256]
        at = comp * 32 + x
        if half == 0:
            into_first = pltpu.roll(edge_in[0], (128 - at) % 128, 1)
            into_last, here = (pltpu.roll(high, 127, 1), low)
        else:
            into_last = pltpu.roll(edge_in[1], 127 - at, 1)
            into_first, here = (pltpu.roll(low, 1, 1), high)
        ahead = jnp.where(lane == 127, into_last, pltpu.roll(here, 127, 1))
        behind = jnp.where(lane == 0, into_first, pltpu.roll(here, 1, 1))
        return ahead - behind

    def first_diff(comp, x, half):
        lanes = slice(half * 128, half * 128 + 128)
        return vel[comp, x + 2, :, lanes] - vel[comp, x, :, lanes]

    def level_copy(source, part, origin, kind, target):
        rows = pl.ds(part * 4, 4)
        lanes = pl.ds(pl.multiple_of(origin * 128, 128), 128)
        return pltpu.make_async_remote_copy(
            own.at[rows] if source is None else level.at[rows, :, lanes],
            level.at[rows, :, lanes],
            level_send.at[kind, origin // 2, part],
            level_recv.at[origin, part],
            device_id={"gz": target},
        )

    def own_copy(part):
        lanes = pl.ds(pl.multiple_of(gz * 128, 128), 128)
        return pltpu.make_async_copy(
            own.at[pl.ds(part * 4, 4)], level.at[pl.ds(part * 4, 4), :, lanes], own_sem.at[0, part]
        )

    def piece_copy(mask, part):
        target = flip(gz, mask)
        rows = pl.ds(part * 8, 8)
        lanes = pl.ds(pl.multiple_of(gz * 256, 256), 256)
        source = block.at[pl.ds(target * 12, 12), rows, :]
        if mask == 0:
            return pltpu.make_async_copy(source, pencil.at[:, rows, lanes], own_sem.at[1, part])
        return pltpu.make_async_remote_copy(
            source, pencil.at[:, rows, lanes], a2a_send.at[mask, part], a2a_recv.at[mask, part],
            device_id={"gz": target},
        )

    for part in ORDER:
        if part == 0:
            halos[2].wait_recv()
            halos[5].wait_recv()

        def one_plane(i, carry):
            x = part * 8 + i
            for half in (0, 1):
                one = second_diff(W, 1, x, half) - third_diff(V, x, half)
                total = one * one
                two = third_diff(U, x, half) - first_diff(W, x, half)
                total = total + two * two
                three = first_diff(V, x, half) - second_diff(U, 0, x, half)
                total = total + three * three
                planes[i, :, half * 128 : half * 128 + 128] = jnp.sqrt(1.0 + 0.25 * total)
            return carry

        lax.fori_loop(0, GROUP, one_plane, 0)

        def turn(y, carry):
            rows = pl.ds(pl.multiple_of(y * 8, 8), 8)
            for half in (0, 1):
                lanes = slice(half * 128, half * 128 + 128)
                block[rows, part * 8 : part * 8 + 8, lanes] = jnp.swapaxes(
                    planes[:, rows, lanes], 0, 1
                )
            return carry

        lax.fori_loop(0, 12, turn, 0)

        for j in range(4):
            halves[...] = lane_pairs(planes[2 * j] + planes[2 * j + 1], pair)
            even = halves[pl.ds(0, 48, stride=2), :]
            odd = halves[pl.ds(1, 48, stride=2), :]
            own[part * 4 + j] = (even + odd) * 0.125

        @pl.when(chip < 3)
        def _():
            level_copy(None, part, gz, 0, gz + 2).start()

        @pl.when(chip > 0)
        def _():
            level_copy(None, part, gz, 1, gz - 2).start()

        level_copy(None, part, gz, 2, flip(gz, 1)).start()
        for mask in (6, 7, 4, 5, 2, 3, 1, 0):
            piece_copy(mask, part).start()
        own_copy(part).start()

    for hop in (1, 2, 3):
        for part in ORDER:

            @pl.when(chip >= hop)
            def _():
                origin = gz - 2 * hop
                level_copy(None, part, origin, 0, gz).wait_recv()

                @pl.when(chip < 3)
                def _():
                    level_copy(level, part, origin, 0, gz + 2).start()

                level_copy(level, part, origin, 2, flip(gz, 1)).start()

            @pl.when(chip + hop < 4)
            def _():
                origin = gz + 2 * hop
                level_copy(None, part, origin, 1, gz).wait_recv()

                @pl.when(chip > 0)
                def _():
                    level_copy(level, part, origin, 1, gz - 2).start()

                level_copy(level, part, origin, 2, flip(gz, 1)).start()

    for part in ORDER:
        own_copy(part).wait()
        piece_copy(0, part).wait()
        for mask in range(1, 8):
            piece_copy(mask, part).wait()
        for q in range(CHIPS):
            other = 2 * q + 1 - core
            mine = 2 * q + core
            level_copy(level, part, other, 2, flip(gz, 1)).wait_recv()
            level_copy(level, part, mine, 2, flip(gz, 1)).wait_send()

            @pl.when((q <= chip) & (chip < 3))
            def _():
                level_copy(level, part, mine, 0, gz).wait_send()

            @pl.when((q >= chip) & (chip > 0))
            def _():
                level_copy(level, part, mine, 1, gz).wait_send()

    for copy in halos:
        copy.wait_send()


def finish(
    pencil, level, mag_out, one_out, two_out, three_out, four_out, five_out,
    two_half, three_half, four_half, five_half, three_at, four_at, sems,
):
    copies = [
        pltpu.make_async_copy(pencil, mag_out, sems.at[0]),
        pltpu.make_async_copy(level, one_out, sems.at[1]),
    ]
    for copy in copies:
        copy.start()
    pair = pairing()

    def step(low, high, half, rows, lanes):
        summed = low + high
        if lanes >= 256:
            for s in range(lanes // 256):
                half[0:rows, s * 128 : s * 128 + 128] = lane_pairs(
                    summed[:, s * 256 : s * 256 + 256], pair
                )
        else:
            half[0:rows, 0:64] = lane_pairs(summed, pair[0:128, 0:64])
        width = lanes // 2
        even = half[pl.ds(0, rows // 2, stride=2), 0:width]
        odd = half[pl.ds(1, rows // 2, stride=2), 0:width]
        return (even + odd) * 0.125

    for i in range(8):
        for s in range(4):
            summed = level[2 * i, :, s * 256 : s * 256 + 256] + level[2 * i + 1, :, s * 256 : s * 256 + 256]
            two_half[s, :, :] = lane_pairs(summed, pair)
            even = two_half[s, pl.ds(0, 24, stride=2), :]
            odd = two_half[s, pl.ds(1, 24, stride=2), :]
            two_out[i, :, s * 128 : s * 128 + 128] = (even + odd) * 0.125
    for i in range(4):
        for s in range(2):
            lanes = slice(s * 256, s * 256 + 256)
            three_half[...] = lane_pairs(two_out[2 * i, :, lanes] + two_out[2 * i + 1, :, lanes], pair)
            even = three_half[pl.ds(0, 12, stride=2), :]
            odd = three_half[pl.ds(1, 12, stride=2), :]
            value = (even + odd) * 0.125
            three_at[i, :, s * 128 : s * 128 + 128] = value
            for r in range(12):
                three_out[r, i : i + 1, s * 128 : s * 128 + 128] = value[r : r + 1]
    for i in range(2):
        four_half[...] = lane_pairs(three_at[2 * i] + three_at[2 * i + 1], pair)
        value = (four_half[pl.ds(0, 6, stride=2), :] + four_half[pl.ds(1, 6, stride=2), :]) * 0.125
        four_at[i] = value
        for r in range(6):
            four_out[r, i : i + 1, :] = value[r : r + 1]
    five_half[...] = lane_pairs(four_at[0] + four_at[1], pair[0:128, :])
    value = (five_half[pl.ds(0, 3, stride=2), :] + five_half[pl.ds(1, 3, stride=2), :]) * 0.125
    for r in range(3):
        five_out[r] = value[r : r + 1, 0:64]
    for copy in copies:
        copy.wait()


def on_device(velocity):
    dma, vmem = (pltpu.SemaphoreType.DMA, pltpu.VMEM)
    pencil, level = pl.pallas_call(
        exchange,
        name="exchange",
        out_shape=(vmem((12, 32, 2048), F32), vmem((16, 48, 1024), F32)),
        in_specs=[pl.BlockSpec(memory_space=pl.ANY)],
        out_specs=(pl.BlockSpec(memory_space=vmem), pl.BlockSpec(memory_space=vmem)),
        scratch_shapes=[
            vmem((3, 34, 96, 256), F32),
            vmem((8, 96, 256), F32),
            vmem((96, 32, 256), F32),
            vmem((16, 48, 128), F32),
            vmem((96, 128), F32),
            vmem((2, 96, 128), F32),
            vmem((2, 96, 128), F32),
            vmem((2, 2, 32, 2, 128), F32),
            vmem((2, 2, 32, 2, 128), F32),
            dma((3,)),
            dma((2, 2)),
            dma((2, 2)),
            dma((2, 2)),
            dma((8, 4)),
            dma((8, 4)),
            dma((3, 4, 4)),
            dma((8, 4)),
            dma((2, 4)),
            dma((1,)),
        ],
        compiler_params=pltpu.CompilerParams(
            collective_id=0, has_side_effects=True, vmem_limit_bytes=48 * 1024 * 1024
        ),
    )(velocity)
    any_space = pl.BlockSpec(memory_space=pl.ANY)
    local = pl.BlockSpec(memory_space=vmem)
    mag, one, two, three, four, five = pl.pallas_call(
        finish,
        name="finish",
        out_shape=(
            jax.ShapeDtypeStruct((12, 32, 2048), F32),
            jax.ShapeDtypeStruct((16, 48, 1024), F32),
            jax.ShapeDtypeStruct((8, 24, 512), F32),
            jax.ShapeDtypeStruct((12, 4, 256), F32),
            jax.ShapeDtypeStruct((6, 2, 128), F32),
            jax.ShapeDtypeStruct((3, 1, 64), F32),
        ),
        in_specs=[local, local],
        out_specs=(any_space, any_space, local, local, local, local),
        scratch_shapes=[
            vmem((4, 48, 128), F32),
            vmem((24, 128), F32),
            vmem((12, 128), F32),
            vmem((6, 128), F32),
            vmem((4, 12, 256), F32),
            vmem((2, 6, 128), F32),
            dma((2,)),
        ],
    )(pencil, level)
    swap = lambda value: jnp.swapaxes(value, 0, 1)
    return swap(mag), one, two, swap(three), swap(four), swap(five)


def solution(mesh):
    in_specs = (P(None, "gx", "gy", "gz"),)
    out_specs = (
        P("gx", ("gy", "gz"), None),
        P("gx", "gy", None),
        P("gx", "gy", None),
        P("gx", "gy", None),
        P("gx", "gy", None),
        P("gx", "gy", None),
    )
    return jax.shard_map(
        on_device, mesh=mesh, in_specs=in_specs, out_specs=out_specs, check_vma=False
    )
```

time: 288 us -> 127 us (0.44); the launches traced: 282 us -> 126 us
  Pallas kernels: 0 us -> 122 us
  waiting for transfers between devices: 116 us -> 0 us
  local copies, waits for them, and re-layouts: 81.1 us -> 3.3 us
  other arithmetic: 41.7 us -> 0 us
  starting transfers between devices: 19.4 us -> 0 us
  between operations: 14.6 us -> 0.65 us
  matrix products: 9.52 us -> 0 us
    pallas_call x0 -> x2, Pallas kernels: none -> 122 us  [the longest x1 115 us: on_device(): pl.pallas_call(exchange, name='exchange', out_shape=(vmem((12, 32, 2048),...]
    all_to_all x1 -> x0, waiting for transfers between devices: 71.1 us -> none  [on_device(): lax.all_to_all(block_mag, 'gz', split_axis=1, concat_axis=2, tiled=True)]
    all_gather x1 -> x0, waiting for transfers between devices: 44.7 us -> none  [on_device(): level_one = lax.all_gather(pooled(pencil), 'gz', axis=1, tiled=True)]
    unnamed x11 -> x4, local copies, waits for them, and re-layouts: 27.4 us -> 3.3 us
    slice x6 -> x0, local copies, waits for them, and re-layouts: 21.9 us -> none  [the longest x2 10.1 us: depth_diff(): behind = jnp.roll(field, 1, 2)]
    sqrt x1 -> x0, other arithmetic: 21.7 us -> none  [vorticity(): jnp.sqrt(1.0 + curl_first * curl_first + curl_second * curl_second + curl...]
    reduce_sum x7 -> x0, other arithmetic: 17.5 us -> none  [the longest x2 12.4 us: pooled(): summed = field.reshape(rows // 2, 2, cols, depth).sum(axis=1)]
    ppermute x6 -> x0, starting transfers between devices: 15.5 us -> none  [the longest x3 15.4 us: extended(): after = lax.ppermute(leading, axis, down)]
  transfers between devices with their start and end apart: 8 -> 0, of which waited for: 2 -> 0; matrix products, arithmetic and copies ran while one was open for 22% -> 0% of each run, Pallas kernels for 0% -> 0%
where the time goes in v1:
time: 127 us; the launch traced here: 126 us
  Pallas kernels  122 us (96%)
  local copies, waits for them, and re-layouts  3.3 us (3%)
    pallas_call x1, Pallas kernels, on_device(): pl.pallas_call(exchange, name='exchange', out_shape=(vmem((12, 32, 2048),...  115 us
    pallas_call x1, Pallas kernels, on_device(): pl.pallas_call(finish, name='finish', out_shape=(jax.ShapeDtypeStruct((12...  6.41 us
    unnamed x4, local copies, waits for them, and re-layouts  3.3 us

profile of v1, /device:TPU:2, one launch (start us, length us, event | category | flops | bytes accessed | tf_op | source)
XLA Modules:
  0.0 125.6 jit_solution(5284806466553058150)
XLA Ops:
  0.6 115.2 %exchange.1 = (f32[12,32,2048]{2,1,0:T(8,128)S(1)}, f32[16,48,1024]{2,1,0:T(8,128)S(1)}) custom-call(f32[3,32,96,256]{3,2,1,0:T(8,128)} %vel_hbm.1), custom_call_target="tpu_custom_call" | custom-call | tf_op jit(solution)/shard_map/exchange/pallas_call | solution.py:325
  115.9 0.0 copy-start
  115.9 1.6 %copy-done = f32[12,32,2048]{2,1,0:T(8,128)} copy-done((f32[12,32,2048]{2,1,0:T(8,128)}, f32[12,32,2048]{2,1,0:T(8,128)S(1)}, u32[]{:S(2)}) %copy-start) | copy-done | bytes 3145752
  117.5 0.0 copy-start.1
  117.5 1.7 %copy-done.1 = f32[16,48,1024]{2,1,0:T(8,128)} copy-done((f32[16,48,1024]{2,1,0:T(8,128)}, f32[16,48,1024]{2,1,0:T(8,128)S(1)}, u32[]{:S(2)}) %copy-start.1) | copy-done | bytes 3145752
  119.2 6.4 %finish.1 = (f32[12,32,2048]{2,1,0:T(8,128)}, f32[16,48,1024]{2,1,0:T(8,128)}, f32[8,24,512]{2,1,0:T(8,128)}, f32[12,4,256]{2,1,0:T(4,128)}, f32[6,2,128]{2,1,0:T(2,128)}, /*index=5*/f32[3,1,64]{2,1,0:T(1,128)}) custom-call(f32[12,32,2048]{2,1,0:T(8,128)} %copy-done, f32[16,48,1024]{2,1,0:T(8,128)} %copy-done.1), custom_call_target="tpu_custom_call" | custom-call | tf_op jit(solution)/shard_map/finish/pallas_call | solution.py:358
Async XLA Ops:
  115.9 1.6 %copy-start = (f32[12,32,2048]{2,1,0:T(8,128)}, f32[12,32,2048]{2,1,0:T(8,128)S(1)}, u32[]{:S(2)}) copy-start(f32[12,32,2048]{2,1,0:T(8,128)S(1)} %get-tuple-element.14.pencil) | copy-start | bytes 9437188
  117.5 1.7 %copy-start.1 = (f32[16,48,1024]{2,1,0:T(8,128)}, f32[16,48,1024]{2,1,0:T(8,128)S(1)}, u32[]{:S(2)}) copy-start(f32[16,48,1024]{2,1,0:T(8,128)S(1)} %get-tuple-element.15.level) | copy-start | bytes 9437188

commit v2 on v1

v2 whole, which is shorter than its diff:
```python
import functools

import jax
import jax.numpy as jnp
from jax import lax
from jax.experimental import pallas as pl
from jax.experimental.pallas import tpu as pltpu
from jax.sharding import PartitionSpec as P

F32 = jnp.float32
GROUP = 8
ORDER = (1, 2, 0, 3)
U, V, W = (0, 1, 2)


def pairing():
    upper = lax.broadcasted_iota(jnp.int32, (256, 128), 0) // 2
    lower = lax.broadcasted_iota(jnp.int32, (256, 128), 1)
    return (upper == lower).astype(F32)


def lane_pairs(value, pair):
    return jnp.dot(value, pair, precision=lax.Precision.HIGHEST, preferred_element_type=F32)


def flip(index, mask):
    bits = [(index // w) % 2 for w in (1, 2, 4)]
    bits = [1 - b if (mask >> i) % 2 else b for i, b in enumerate(bits)]
    return bits[0] + 2 * bits[1] + 4 * bits[2]


def exchange(
    vel_hbm, pencil, level, vel, planes, block, own, halves, thirds, edge_out, edge_in, row_out,
    row_in, far, load_sem, x_sem, y_sem, z_sem, a2a_send, a2a_recv, send_sem, level_recv, far_recv,
    own_sem,
):
    gx, gy, gz = (lax.axis_index("gx"), lax.axis_index("gy"), lax.axis_index("gz"))
    half = gz // 4
    x_sides = [{"gx": (gx + 3) % 4}, {"gx": (gx + 1) % 4}]
    y_sides = [{"gy": (gy + 7) % 8}, {"gy": (gy + 1) % 8}]
    z_sides = [{"gz": (gz + 7) % 8}, {"gz": (gz + 1) % 8}]

    def load(comp, part):
        return pltpu.make_async_copy(
            vel_hbm.at[comp, pl.ds(part * 8, 8)],
            vel.at[comp, pl.ds(part * 8 + 1, 8), 8:104],
            load_sem.at[comp, part],
        )

    for part in range(4):
        load(U, part).start()
        load(V, part).start()
    for part in range(4):
        load(W, part).start()

    barrier = pltpu.get_barrier_semaphore()
    for mask in range(1, 8):
        pl.semaphore_signal(barrier, inc=1, device_id={"gz": flip(gz, mask)})
    for side in x_sides + y_sides:
        pl.semaphore_signal(barrier, inc=1, device_id=side)

    lane = lax.broadcasted_iota(jnp.int32, (96, 128), 1)

    def pack_edges(x, carry):
        first, last = carry
        for comp in (U, V):
            at = comp * 32 + x
            low, high = (vel[comp, x + 1, 8:104, 0:128], vel[comp, x + 1, 8:104, 128:256])
            first = jnp.where(lane == at, pltpu.roll(low, at, 1), first)
            last = jnp.where(lane == at, pltpu.roll(high, at + 1, 1), last)
        return first, last

    edges = (jnp.zeros((96, 128), F32), jnp.zeros((96, 128), F32))
    for part in range(4):
        load(U, part).wait()
        load(V, part).wait()
        edges = lax.fori_loop(part * 8, part * 8 + 8, pack_edges, edges)
    edge_out[0] = edges[0]
    edge_out[1] = edges[1]

    z_halos, y_halos, x_halos = ([], [], [])
    for side in (0, 1):
        z_halos.append(
            pltpu.make_async_remote_copy(
                edge_out.at[side], edge_in.at[1 - side], z_sem.at[0, side], z_sem.at[1, 1 - side],
                device_id=z_sides[side],
            )
        )
        y_halos.append(
            pltpu.make_async_remote_copy(
                row_out.at[side], row_in.at[1 - side], y_sem.at[0, side], y_sem.at[1, 1 - side],
                device_id=y_sides[side],
            )
        )
        x_halos.append(
            pltpu.make_async_remote_copy(
                vel.at[1:3, 31 * side + 1, 8:104], vel.at[1:3, 33 - 33 * side, 8:104],
                x_sem.at[0, side], x_sem.at[1, 1 - side], device_id=x_sides[side],
            )
        )
    pl.semaphore_wait(barrier, 11)
    for copy in z_halos:
        copy.start()

    def pack_rows(x, carry):
        for spot, comp in enumerate((U, W)):
            for h in (0, 1):
                lanes = slice(h * 128, h * 128 + 128)
                row_out[0, spot, x, h : h + 1, :] = vel[comp, x + 1, 8:9, lanes]
                row_out[1, spot, x, h : h + 1, :] = vel[comp, x + 1, 103:104, lanes]
        return carry

    for part in range(4):
        load(W, part).wait()
    lax.fori_loop(0, 32, pack_rows, 0)
    for copy in y_halos + x_halos:
        copy.start()
    for copy in z_halos:
        copy.wait_recv()

    pair = pairing()

    def magnitude_rows(x, start, count):
        rows = pl.ds(pl.multiple_of(start, 8), count)
        inner = pl.ds(pl.multiple_of(start + 8, 8), count)
        outer = pl.ds(pl.multiple_of(start, 8), count + 16)
        column = lax.broadcasted_iota(jnp.int32, (count, 128), 1)

        for h in (0, 1):
            lanes = slice(h * 128, h * 128 + 128)

            def second_diff(comp):
                value = vel[comp, x + 1, outer, lanes]
                ahead = pltpu.roll(value, count + 15, 0)
                behind = pltpu.roll(value, 1, 0)
                return (ahead - behind)[8 : 8 + count]

            def third_diff(comp):
                low = vel[comp, x + 1, inner, 0:128]
                high = vel[comp, x + 1, inner, 128:256]
                at = comp * 32 + x
                if h == 0:
                    into_first = pltpu.roll(edge_in[0, rows, :], (128 - at) % 128, 1)
                    into_last, here = (pltpu.roll(high, 127, 1), low)
                else:
                    into_last = pltpu.roll(edge_in[1, rows, :], 127 - at, 1)
                    into_first, here = (pltpu.roll(low, 1, 1), high)
                ahead = jnp.where(column == 127, into_last, pltpu.roll(here, 127, 1))
                behind = jnp.where(column == 0, into_first, pltpu.roll(here, 1, 1))
                return ahead - behind

            def first_diff(comp):
                return vel[comp, x + 2, inner, lanes] - vel[comp, x, inner, lanes]

            one = second_diff(W) - third_diff(V)
            total = one * one
            two = third_diff(U) - first_diff(W)
            total = total + two * two
            three = first_diff(V) - second_diff(U)
            total = total + three * three
            planes[x, rows, lanes] = jnp.sqrt(1.0 + 0.25 * total)

    def make_rows(part, start, count):
        def one_plane(i, carry):
            magnitude_rows(part * 8 + i, start, count)
            return carry

        lax.fori_loop(0, GROUP, one_plane, 0)

        def turn(y, carry):
            rows = pl.ds(pl.multiple_of(start + y * 8, 8), 8)
            for h in (0, 1):
                lanes = slice(h * 128, h * 128 + 128)
                block[rows, part * 8 : part * 8 + 8, lanes] = jnp.swapaxes(
                    planes[part * 8 : part * 8 + 8, rows, lanes], 0, 1
                )
            return carry

        lax.fori_loop(0, count // 8, turn, 0)

    def piece_copy(mask, part):
        target = flip(gz, mask)
        rows = pl.ds(part * 8, 8)
        lanes = pl.ds(pl.multiple_of(gz * 256, 256), 256)
        source = block.at[pl.ds(target * 12, 12), rows, :]
        if mask == 0:
            return pltpu.make_async_copy(source, pencil.at[:, rows, lanes], own_sem.at[1, part])
        return pltpu.make_async_remote_copy(
            source, pencil.at[:, rows, lanes], a2a_send.at[mask, part], a2a_recv.at[mask, part],
            device_id={"gz": target},
        )

    def send_pieces(masks, part, inner):
        for mask in masks:
            target = flip(gz, mask)
            interior = (target > 0) & (target < 7)

            @pl.when(interior if inner else jnp.logical_not(interior))
            def _():
                piece_copy(mask, part).start()

    FAR, NEAR = ((6, 7, 4, 5), (2, 3, 1, 0))
    far_start, near_start = ((1 - half) * 48, half * 48)

    def level_copy(kind, part, origin, target, mine=False):
        every = kind < 3
        first = 0 if every else pl.multiple_of((origin // 4) * 24, 8)
        rows = pl.ds(first, 48 if every else 24)
        parts = pl.ds(part * 4, 4)
        lanes = pl.ds(pl.multiple_of(origin * 128, 128), 128)
        place = level.at[parts, rows, lanes]
        return pltpu.make_async_remote_copy(
            own.at[parts, rows] if mine else place, place,
            send_sem.at[kind, part], level_recv.at[origin, part], device_id={"gz": target},
        )

    def far_copy(kind, part, origin, target):
        place = far.at[origin % 4, pl.ds(part * 4, 4)]
        return pltpu.make_async_remote_copy(
            place, place, send_sem.at[kind, part], far_recv.at[origin % 4, part],
            device_id={"gz": target},
        )

    def own_copy(part):
        lanes = pl.ds(pl.multiple_of(gz * 128, 128), 128)
        return pltpu.make_async_copy(
            own.at[pl.ds(part * 4, 4)], level.at[pl.ds(part * 4, 4), :, lanes], own_sem.at[0, part]
        )

    mate, beside, across, past = (flip(gz, 1), flip(gz, 2), flip(gz, 6), flip(gz, 4))

    for part in ORDER:
        if part == 0:
            for copy in x_halos:
                copy.wait_recv()
        make_rows(part, far_start, 48)
        if part != 3:
            send_pieces(FAR, part, True)
        make_rows(part, near_start, 48)
        if part != 3:
            send_pieces(NEAR, part, True)

    for copy in y_halos:
        copy.wait_recv()

    def fill_rows(x, carry):
        for spot, comp in enumerate((U, W)):
            for h in (0, 1):
                lanes = slice(h * 128, h * 128 + 128)
                vel[comp, x + 1, 7:8, lanes] = row_in[0, spot, x, h : h + 1, :]
                vel[comp, x + 1, 104:105, lanes] = row_in[1, spot, x, h : h + 1, :]
        return carry

    lax.fori_loop(0, 32, fill_rows, 0)
    for part in ORDER:
        make_rows(part, 0, 8)
        make_rows(part, 88, 8)
        for j in range(part * 4, part * 4 + 4):
            halves[...] = lane_pairs(planes[2 * j] + planes[2 * j + 1], pair)
            even = halves[pl.ds(0, 48, stride=2), :]
            odd = halves[pl.ds(1, 48, stride=2), :]
            own[j] = (even + odd) * 0.125
        level_copy(3, part, gz, across, True).start()
        level_copy(1, part, gz, beside, True).start()
        level_copy(0, part, gz, mate, True).start()
        own_copy(part).start()
    for part in ORDER:
        send_pieces(FAR + NEAR, part, False)
        if part == 3:
            send_pieces(FAR + NEAR, part, True)

    def pass_far(part):
        for mask in FAR:
            piece_copy(mask, part).wait_recv()
        parts = pl.ds(part * 8, 8)
        for s in range(4):
            lanes = pl.ds(pl.multiple_of((1 - half) * 1024 + s * 256, 256), 256)
            rows = [pencil[2 * r, parts, lanes] + pencil[2 * r + 1, parts, lanes] for r in range(6)]
            thirds[s] = lane_pairs(jnp.concatenate(rows, axis=0), pair)
            for j in range(4):
                even = thirds[s, pl.ds(2 * j, 6, stride=8), :]
                odd = thirds[s, pl.ds(2 * j + 1, 6, stride=8), :]
                far[gz % 4, part * 4 + j, 0:6, s * 128 : s * 128 + 128] = (even + odd) * 0.125
        far_copy(8, part, gz, beside).start()
        far_copy(7, part, gz, mate).start()

    def pass_level(part):
        level_copy(3, part, across, across).wait_recv()
        level_copy(4, part, across, beside).start()
        level_copy(5, part, across, mate).start()

    for part in ORDER:
        level_copy(1, part, beside, beside).wait_recv()
        level_copy(2, part, beside, mate).start()
    for part in ORDER[:3]:
        pass_far(part)
    for part in ORDER:
        pass_level(part)
    for part in ORDER[:3]:
        far_copy(8, part, beside, beside).wait_recv()
        far_copy(9, part, beside, mate).start()
    for part in ORDER:
        level_copy(4, part, past, beside).wait_recv()
        level_copy(6, part, past, mate).start()
    pass_far(3)
    far_copy(8, 3, beside, beside).wait_recv()
    far_copy(9, 3, beside, mate).start()

    for part in ORDER:
        own_copy(part).wait()
        piece_copy(0, part).wait()
        for mask in range(1, 8):
            piece_copy(mask, part).wait_send()
        for mask in (1, 2, 3):
            piece_copy(mask, part).wait_recv()
        level_copy(0, part, mate, mate).wait_recv()
        level_copy(2, part, flip(gz, 3), mate).wait_recv()
        level_copy(5, part, flip(gz, 7), mate).wait_recv()
        level_copy(6, part, flip(gz, 5), mate).wait_recv()
        far_copy(7, part, mate, mate).wait_recv()
        far_copy(9, part, flip(gz, 3), mate).wait_recv()

    for side in (0, 1):

        @pl.when(half == side)
        def _():
            for d in range(4):
                rows = slice(side * 24 + d * 6, side * 24 + d * 6 + 6)
                lanes = slice((1 - side) * 512, (1 - side) * 512 + 512)

                def place_rows(j, carry):
                    level[j, rows, lanes] = far[d, j, 0:6, :]
                    return carry

                lax.fori_loop(0, 16, place_rows, 0)

    for part in ORDER:
        level_copy(0, part, gz, mate).wait_send()
        level_copy(1, part, gz, beside).wait_send()
        level_copy(2, part, beside, mate).wait_send()
        level_copy(3, part, gz, across).wait_send()
        level_copy(4, part, across, beside).wait_send()
        level_copy(5, part, across, mate).wait_send()
        level_copy(6, part, past, mate).wait_send()
        far_copy(7, part, gz, mate).wait_send()
        far_copy(8, part, gz, beside).wait_send()
        far_copy(9, part, beside, mate).wait_send()
    for copy in z_halos + y_halos + x_halos:
        copy.wait_send()


def finish(
    pencil, level, mag_out, one_out, two_out, three_out, four_out, five_out,
    two_half, three_half, four_half, five_half, three_at, four_at, sems,
):
    copies = [
        pltpu.make_async_copy(pencil, mag_out, sems.at[0]),
        pltpu.make_async_copy(level, one_out, sems.at[1]),
    ]
    for copy in copies:
        copy.start()
    pair = pairing()

    def step(low, high, half, rows, lanes):
        summed = low + high
        if lanes >= 256:
            for s in range(lanes // 256):
                half[0:rows, s * 128 : s * 128 + 128] = lane_pairs(
                    summed[:, s * 256 : s * 256 + 256], pair
                )
        else:
            half[0:rows, 0:64] = lane_pairs(summed, pair[0:128, 0:64])
        width = lanes // 2
        even = half[pl.ds(0, rows // 2, stride=2), 0:width]
        odd = half[pl.ds(1, rows // 2, stride=2), 0:width]
        return (even + odd) * 0.125

    for i in range(8):
        for s in range(4):
            summed = level[2 * i, :, s * 256 : s * 256 + 256] + level[2 * i + 1, :, s * 256 : s * 256 + 256]
            two_half[s, :, :] = lane_pairs(summed, pair)
            even = two_half[s, pl.ds(0, 24, stride=2), :]
            odd = two_half[s, pl.ds(1, 24, stride=2), :]
            two_out[i, :, s * 128 : s * 128 + 128] = (even + odd) * 0.125
    for i in range(4):
        for s in range(2):
            lanes = slice(s * 256, s * 256 + 256)
            three_half[...] = lane_pairs(two_out[2 * i, :, lanes] + two_out[2 * i + 1, :, lanes], pair)
            even = three_half[pl.ds(0, 12, stride=2), :]
            odd = three_half[pl.ds(1, 12, stride=2), :]
            value = (even + odd) * 0.125
            three_at[i, :, s * 128 : s * 128 + 128] = value
            for r in range(12):
                three_out[r, i : i + 1, s * 128 : s * 128 + 128] = value[r : r + 1]
    for i in range(2):
        four_half[...] = lane_pairs(three_at[2 * i] + three_at[2 * i + 1], pair)
        value = (four_half[pl.ds(0, 6, stride=2), :] + four_half[pl.ds(1, 6, stride=2), :]) * 0.125
        four_at[i] = value
        for r in range(6):
            four_out[r, i : i + 1, :] = value[r : r + 1]
    five_half[...] = lane_pairs(four_at[0] + four_at[1], pair[0:128, :])
    value = (five_half[pl.ds(0, 3, stride=2), :] + five_half[pl.ds(1, 3, stride=2), :]) * 0.125
    for r in range(3):
        five_out[r] = value[r : r + 1, 0:64]
    for copy in copies:
        copy.wait()


def on_device(velocity):
    dma, vmem = (pltpu.SemaphoreType.DMA, pltpu.VMEM)
    pencil, level = pl.pallas_call(
        exchange,
        name="exchange",
        out_shape=(vmem((12, 32, 2048), F32), vmem((16, 48, 1024), F32)),
        in_specs=[pl.BlockSpec(memory_space=pl.ANY)],
        out_specs=(pl.BlockSpec(memory_space=vmem), pl.BlockSpec(memory_space=vmem)),
        scratch_shapes=[
            vmem((3, 34, 112, 256), F32),
            vmem((32, 96, 256), F32),
            vmem((96, 32, 256), F32),
            vmem((16, 48, 128), F32),
            vmem((96, 128), F32),
            vmem((4, 48, 128), F32),
            vmem((2, 96, 128), F32),
            vmem((2, 96, 128), F32),
            vmem((2, 2, 32, 2, 128), F32),
            vmem((2, 2, 32, 2, 128), F32),
            vmem((4, 16, 8, 512), F32),
            dma((3, 4)),
            dma((2, 2)),
            dma((2, 2)),
            dma((2, 2)),
            dma((8, 4)),
            dma((8, 4)),
            dma((10, 4)),
            dma((8, 4)),
            dma((4, 4)),
            dma((2, 4)),
        ],
        compiler_params=pltpu.CompilerParams(
            collective_id=0, has_side_effects=True, vmem_limit_bytes=48 * 1024 * 1024
        ),
    )(velocity)
    any_space = pl.BlockSpec(memory_space=pl.ANY)
    local = pl.BlockSpec(memory_space=vmem)
    mag, one, two, three, four, five = pl.pallas_call(
        finish,
        name="finish",
        out_shape=(
            jax.ShapeDtypeStruct((12, 32, 2048), F32),
            jax.ShapeDtypeStruct((16, 48, 1024), F32),
            jax.ShapeDtypeStruct((8, 24, 512), F32),
            jax.ShapeDtypeStruct((12, 4, 256), F32),
            jax.ShapeDtypeStruct((6, 2, 128), F32),
            jax.ShapeDtypeStruct((3, 1, 64), F32),
        ),
        in_specs=[local, local],
        out_specs=(any_space, any_space, local, local, local, local),
        scratch_shapes=[
            vmem((4, 48, 128), F32),
            vmem((24, 128), F32),
            vmem((12, 128), F32),
            vmem((6, 128), F32),
            vmem((4, 12, 256), F32),
            vmem((2, 6, 128), F32),
            dma((2,)),
        ],
        compiler_params=pltpu.CompilerParams(vmem_limit_bytes=16 * 1024 * 1024),
    )(pltpu.with_memory_space_constraint(pencil, vmem), pltpu.with_memory_space_constraint(level, vmem))
    swap = lambda value: jnp.swapaxes(value, 0, 1)
    return swap(mag), one, two, swap(three), swap(four), swap(five)


def solution(mesh):
    in_specs = (P(None, "gx", "gy", "gz"),)
    out_specs = (
        P("gx", ("gy", "gz"), None),
        P("gx", "gy", None),
        P("gx", "gy", None),
        P("gx", "gy", None),
        P("gx", "gy", None),
        P("gx", "gy", None),
    )
    return jax.shard_map(
        on_device, mesh=mesh, in_specs=in_specs, out_specs=out_specs, check_vma=False
    )
```

time: 127 us -> 103 us (0.81)
  Pallas kernels: 122 us -> 101 us
  local copies, waits for them, and re-layouts: 3.3 us -> 0 us
    pallas_call x1, Pallas kernels: 115 us -> 97.1 us  [on_device(): pl.pallas_call(exchange, name='exchange', out_shape=(vmem((12, 32, 2048),...]
    unnamed x4 -> x0, local copies, waits for them, and re-layouts: 3.3 us -> none
    pallas_call x1, Pallas kernels: 6.41 us -> 3.54 us  [on_device(): pl.pallas_call(finish, name='finish', out_shape=(jax.ShapeDtypeStruct((12...]
where the time goes in v2:
time: 103 us; the launch traced here: 101 us
  Pallas kernels  101 us (98%)
    pallas_call x1, Pallas kernels, on_device(): pl.pallas_call(exchange, name='exchange', out_shape=(vmem((12, 32, 2048),...  97.1 us
    pallas_call x1, Pallas kernels, on_device(): pl.pallas_call(finish, name='finish', out_shape=(jax.ShapeDtypeStruct((12...  3.54 us

profile of v2, /device:TPU:2, one launch (start us, length us, event | category | flops | bytes accessed | tf_op | source)
XLA Modules:
  0.0 101.2 jit_solution(9462737993301836347)
XLA Ops:
  0.6 97.1 %exchange.1 = (f32[12,32,2048]{2,1,0:T(8,128)S(1)}, f32[16,48,1024]{2,1,0:T(8,128)S(1)}) custom-call(f32[3,32,96,256]{3,2,1,0:T(8,128)} %vel_hbm.1), custom_call_target="tpu_custom_call" | custom-call | tf_op jit(solution)/shard_map/exchange/pallas_call | solution.py:411
  97.7 3.5 %finish.1 = (f32[12,32,2048]{2,1,0:T(8,128)}, f32[16,48,1024]{2,1,0:T(8,128)}, f32[8,24,512]{2,1,0:T(8,128)}, f32[12,4,256]{2,1,0:T(4,128)}, f32[6,2,128]{2,1,0:T(2,128)}, /*index=5*/f32[3,1,64]{2,1,0:T(1,128)}) custom-call(f32[12,32,2048]{2,1,0:T(8,128)S(1)} %get-tuple-element.14.pencil, f32[16,48,1024]{2,1,0:T(8,128)S(1)} %get-tuple-element.15.level), custom_call_target="tpu_custom_call" | custom-call | tf_op jit(solution)/shard_map/finish/pallas_call | solution.py:446

commit v3 on v2

--- a/solution.py
+++ b/solution.py
@@ -23,6 +23,18 @@
     return jnp.dot(value, pair, precision=lax.Precision.HIGHEST, preferred_element_type=F32)
 
 
+def lane_pairs_split(value, pair):
+    count = value.shape[0]
+    high = value.astype(jnp.bfloat16)
+    rest = value - high.astype(F32)
+    middle = rest.astype(jnp.bfloat16)
+    low = (rest - middle.astype(F32)).astype(jnp.bfloat16)
+    sums = jnp.dot(
+        jnp.concatenate([high, middle, low], axis=0), pair, preferred_element_type=F32
+    )
+    return sums[0:count] + (sums[count : 2 * count] + sums[2 * count : 3 * count])
+
+
 def flip(index, mask):
     bits = [(index // w) % 2 for w in (1, 2, 4)]
     bits = [1 - b if (mask >> i) % 2 else b for i, b in enumerate(bits)]
@@ -31,33 +43,83 @@
 
 def exchange(
     vel_hbm, pencil, level, vel, planes, block, own, halves, thirds, edge_out, edge_in, row_out,
-    row_in, far, load_sem, x_sem, y_sem, z_sem, a2a_send, a2a_recv, send_sem, level_recv, far_recv,
+    row_in, far, early, patch_out, patch_in, edge_rows, patch_sem, edge_sem, load_sem, x_sem, y_sem, z_sem, a2a_send, a2a_recv, send_sem, level_recv, far_recv,
     own_sem,
 ):
     gx, gy, gz = (lax.axis_index("gx"), lax.axis_index("gy"), lax.axis_index("gz"))
     half = gz // 4
+    FAR, NEAR = ((4, 5, 6, 7), (2, 3, 1, 0))
+    far_start, near_start = ((1 - half) * 48, half * 48)
+    inside = (gz > 0) & (gz < 7)
     x_sides = [{"gx": (gx + 3) % 4}, {"gx": (gx + 1) % 4}]
     y_sides = [{"gy": (gy + 7) % 8}, {"gy": (gy + 1) % 8}]
     z_sides = [{"gz": (gz + 7) % 8}, {"gz": (gz + 1) % 8}]
 
-    def load(comp, part):
+    def load(comp, chunk):
+        at, planes_in = ((7, 10), (0, 7), (17, 15))[chunk]
+        first, count = (0, 96) if comp == V else (8, 80)
         return pltpu.make_async_copy(
-            vel_hbm.at[comp, pl.ds(part * 8, 8)],
-            vel.at[comp, pl.ds(part * 8 + 1, 8), 8:104],
-            load_sem.at[comp, part],
-        )
-
-    for part in range(4):
-        load(U, part).start()
-        load(V, part).start()
-    for part in range(4):
-        load(W, part).start()
+            vel_hbm.at[comp, at : at + planes_in, first : first + count],
+            vel.at[comp, at + 1 : at + 1 + planes_in, first + 8 : first + 8 + count],
+            load_sem.at[comp, chunk],
+        )
+
+    def load_side(comp, side):
+        return pltpu.make_async_copy(
+            vel_hbm.at[comp, :, side * 88 : side * 88 + 8],
+            vel.at[comp, 1:33, side * 88 + 8 : side * 88 + 16],
+            load_sem.at[3, comp + side],
+        )
+
+    sides = [load_side(comp, side) for comp in (U, W) for side in (0, 1)]
+    firsts = [load(comp, 0) for comp in (U, V, W)]
+    seconds = [load(comp, chunk) for chunk in (1, 2) for comp in (U, V)]
+    thirds_in = [load(W, chunk) for chunk in (1, 2)]
+    for copy in sides + firsts + seconds + thirds_in:
+        copy.start()
 
     barrier = pltpu.get_barrier_semaphore()
     for mask in range(1, 8):
         pl.semaphore_signal(barrier, inc=1, device_id={"gz": flip(gz, mask)})
-    for side in x_sides + y_sides:
+    for side in x_sides:
         pl.semaphore_signal(barrier, inc=1, device_id=side)
+    opens = [gy >= 4, (gy < 3) | (gy == 7)]
+    for side in (0, 1):
+
+        @pl.when(jnp.logical_not(opens[side]))
+        def _():
+            pl.semaphore_signal(barrier, inc=1, device_id=y_sides[side])
+
+    greeted = 9 + opens[0].astype(jnp.int32) + opens[1].astype(jnp.int32)
+
+    z_halos, y_halos, x_halos = ([], [], [])
+    for side in (0, 1):
+        z_halos.append(
+            pltpu.make_async_remote_copy(
+                edge_out.at[side], edge_in.at[1 - side], z_sem.at[0, side], z_sem.at[1, 1 - side],
+                device_id=z_sides[side],
+            )
+        )
+        y_halos.append(
+            pltpu.make_async_remote_copy(
+                row_out.at[side], row_in.at[1 - side], y_sem.at[0, side], y_sem.at[1, 1 - side],
+                device_id=y_sides[side],
+            )
+        )
+        x_halos.append(
+            pltpu.make_async_remote_copy(
+                vel.at[1:3, 31 * side + 1, 8:104], vel.at[1:3, 33 - 33 * side, 8:104],
+                x_sem.at[0, side], x_sem.at[1, 1 - side], device_id=x_sides[side],
+            )
+        )
+
+    def pack_rows(x, carry):
+        for spot, comp in enumerate((U, W)):
+            for h in (0, 1):
+                lanes = slice(h * 128, h * 128 + 128)
+                row_out[0, spot, x, h : h + 1, :] = vel[comp, x + 1, 8:9, lanes]
+                row_out[1, spot, x, h : h + 1, :] = vel[comp, x + 1, 103:104, lanes]
+        return carry
 
     lane = lax.broadcasted_iota(jnp.int32, (96, 128), 1)
 
@@ -70,57 +132,19 @@
             last = jnp.where(lane == at, pltpu.roll(high, at + 1, 1), last)
         return first, last
 
-    edges = (jnp.zeros((96, 128), F32), jnp.zeros((96, 128), F32))
-    for part in range(4):
-        load(U, part).wait()
-        load(V, part).wait()
-        edges = lax.fori_loop(part * 8, part * 8 + 8, pack_edges, edges)
-    edge_out[0] = edges[0]
-    edge_out[1] = edges[1]
-
-    z_halos, y_halos, x_halos = ([], [], [])
+    for copy in sides:
+        copy.wait()
+    lax.fori_loop(0, 32, pack_rows, 0)
+    pl.semaphore_wait(barrier, greeted)
     for side in (0, 1):
-        z_halos.append(
-            pltpu.make_async_remote_copy(
-                edge_out.at[side], edge_in.at[1 - side], z_sem.at[0, side], z_sem.at[1, 1 - side],
-                device_id=z_sides[side],
-            )
-        )
-        y_halos.append(
-            pltpu.make_async_remote_copy(
-                row_out.at[side], row_in.at[1 - side], y_sem.at[0, side], y_sem.at[1, 1 - side],
-                device_id=y_sides[side],
-            )
-        )
-        x_halos.append(
-            pltpu.make_async_remote_copy(
-                vel.at[1:3, 31 * side + 1, 8:104], vel.at[1:3, 33 - 33 * side, 8:104],
-                x_sem.at[0, side], x_sem.at[1, 1 - side], device_id=x_sides[side],
-            )
-        )
-    pl.semaphore_wait(barrier, 11)
-    for copy in z_halos:
-        copy.start()
-
-    def pack_rows(x, carry):
-        for spot, comp in enumerate((U, W)):
-            for h in (0, 1):
-                lanes = slice(h * 128, h * 128 + 128)
-                row_out[0, spot, x, h : h + 1, :] = vel[comp, x + 1, 8:9, lanes]
-                row_out[1, spot, x, h : h + 1, :] = vel[comp, x + 1, 103:104, lanes]
-        return carry
-
-    for part in range(4):
-        load(W, part).wait()
-    lax.fori_loop(0, 32, pack_rows, 0)
-    for copy in y_halos + x_halos:
-        copy.start()
-    for copy in z_halos:
-        copy.wait_recv()
-
-    pair = pairing()
-
-    def magnitude_rows(x, start, count):
+
+        @pl.when(opens[side])
+        def _():
+            y_halos[side].start()
+
+    pair = pairing().astype(jnp.bfloat16)
+
+    def magnitude_rows(x, start, count, edged):
         rows = pl.ds(pl.multiple_of(start, 8), count)
         inner = pl.ds(pl.multiple_of(start + 8, 8), count)
         outer = pl.ds(pl.multiple_of(start, 8), count + 16)
@@ -140,10 +164,10 @@
                 high = vel[comp, x + 1, inner, 128:256]
                 at = comp * 32 + x
                 if h == 0:
-                    into_first = pltpu.roll(edge_in[0, rows, :], (128 - at) % 128, 1)
+                    into_first = pltpu.roll(edge_in[0, rows, :], (128 - at) % 128, 1) if edged else 0.0
                     into_last, here = (pltpu.roll(high, 127, 1), low)
                 else:
-                    into_last = pltpu.roll(edge_in[1, rows, :], 127 - at, 1)
+                    into_last = pltpu.roll(edge_in[1, rows, :], 127 - at, 1) if edged else 0.0
                     into_first, here = (pltpu.roll(low, 1, 1), high)
                 ahead = jnp.where(column == 127, into_last, pltpu.roll(here, 127, 1))
                 behind = jnp.where(column == 0, into_first, pltpu.roll(here, 1, 1))
@@ -160,9 +184,9 @@
             total = total + three * three
             planes[x, rows, lanes] = jnp.sqrt(1.0 + 0.25 * total)
 
-    def make_rows(part, start, count):
+    def make_rows(part, start, count, edged=True, side=None):
         def one_plane(i, carry):
-            magnitude_rows(part * 8 + i, start, count)
+            magnitude_rows(part * 8 + i, start, count, edged)
             return carry
 
         lax.fori_loop(0, GROUP, one_plane, 0)
@@ -171,39 +195,121 @@
             rows = pl.ds(pl.multiple_of(start + y * 8, 8), 8)
             for h in (0, 1):
                 lanes = slice(h * 128, h * 128 + 128)
-                block[rows, part * 8 : part * 8 + 8, lanes] = jnp.swapaxes(
-                    planes[part * 8 : part * 8 + 8, rows, lanes], 0, 1
-                )
+                value = jnp.swapaxes(planes[part * 8 : part * 8 + 8, rows, lanes], 0, 1)
+                if side is not None:
+                    edge_rows[side, part * 8 : part * 8 + 8, lanes] = value[7 * side]
+                elif edged:
+                    block[rows, part * 8 : part * 8 + 8, lanes] = value
+                else:
+                    spot = pl.ds(pl.multiple_of(start - far_start + y * 8, 8), 8)
+                    early[spot, :, lanes] = value
             return carry
 
         lax.fori_loop(0, count // 8, turn, 0)
 
-    def piece_copy(mask, part):
+    def piece_copy(mask, part, edge, first=False):
         target = flip(gz, mask)
         rows = pl.ds(part * 8, 8)
         lanes = pl.ds(pl.multiple_of(gz * 256, 256), 256)
-        source = block.at[pl.ds(target * 12, 12), rows, :]
+        skip = (target == 0).astype(jnp.int32) if edge else 0
+        count = 11 if edge else 12
+        source = block.at[pl.ds(target * 12 + skip, count), rows, :]
+        if first:
+            source = early.at[pl.ds((target % 4) * 12 + skip, count)]
+        place = pencil.at[pl.ds(skip, count), rows, lanes]
         if mask == 0:
-            return pltpu.make_async_copy(source, pencil.at[:, rows, lanes], own_sem.at[1, part])
+            return pltpu.make_async_copy(source, place, own_sem.at[1, part])
         return pltpu.make_async_remote_copy(
-            source, pencil.at[:, rows, lanes], a2a_send.at[mask, part], a2a_recv.at[mask, part],
+            source, place, a2a_send.at[mask, part], a2a_recv.at[mask, part],
             device_id={"gz": target},
         )
 
-    def send_pieces(masks, part, inner):
+    def row_copy(mask):
+        target = flip(gz, mask)
+        high = (target == 7).astype(jnp.int32)
+        lanes = pl.ds(pl.multiple_of(gz * 256, 256), 256)
+        source = edge_rows.at[pl.ds(high, 1), :, :]
+        place = pencil.at[pl.ds(11 * high, 1), :, lanes]
+        if mask == 0:
+            return pltpu.make_async_copy(source, place, edge_sem.at[0, 0])
+        return pltpu.make_async_remote_copy(
+            source, place, edge_sem.at[0, mask], edge_sem.at[1, mask], device_id={"gz": target}
+        )
+
+    def either(interior, act):
+        @pl.when(interior)
+        def _():
+            act(False)
+
+        @pl.when(jnp.logical_not(interior))
+        def _():
+            act(True)
+
+    def inner(target):
+        return (target > 0) & (target < 7)
+
+    def piece_arrives(mask, part):
+        either(inside, lambda edge: piece_copy(mask, part, edge).wait_recv())
+
+    def rows_arrive(masks):
+        @pl.when(jnp.logical_not(inside))
+        def _():
+            for mask in masks:
+                row_copy(mask).wait_recv()
+
+    def patch_copy(mask):
+        return pltpu.make_async_remote_copy(
+            patch_out.at[mask - 4], patch_in.at[mask - 4],
+            patch_sem.at[0, mask - 4], patch_sem.at[1, mask - 4], device_id={"gz": flip(gz, mask)},
+        )
+
+    column8 = lax.broadcasted_iota(jnp.int32, (8, 128), 1)
+
+    def send_patches():
+        for mask in FAR:
+            target = flip(gz, mask)
+            patch = jnp.zeros((8, 128), F32)
+            for r in range(12):
+                low = block[target * 12 + r, 8:16, 0:128]
+                high = block[target * 12 + r, 8:16, 128:256]
+                patch = jnp.where(column8 == 2 * r, pltpu.roll(low, 2 * r, 1), patch)
+                patch = jnp.where(column8 == 2 * r + 1, pltpu.roll(high, 2 * r + 2, 1), patch)
+            patch_out[mask - 4] = patch
+            patch_copy(mask).start()
+
+    def apply_patches():
+        for mask in FAR:
+            source = flip(gz, mask)
+            low = pl.ds(pl.multiple_of(source * 256, 128), 128)
+            high = pl.ds(pl.multiple_of(source * 256 + 128, 128), 128)
+            patch_copy(mask).wait_recv()
+            patch = patch_in[mask - 4]
+
+            def patch_row(r):
+                into_low = pltpu.roll(patch, (128 - 2 * r) % 128, 1)
+                into_high = pltpu.roll(patch, 126 - 2 * r, 1)
+                pencil[r, 8:16, low] = jnp.where(column8 == 0, into_low, pencil[r, 8:16, low])
+                pencil[r, 8:16, high] = jnp.where(column8 == 127, into_high, pencil[r, 8:16, high])
+
+            for r in range(1, 11):
+                patch_row(r)
+
+            @pl.when(gz > 0)
+            def _():
+                patch_row(0)
+
+            @pl.when(gz < 7)
+            def _():
+                patch_row(11)
+
+    def send_pieces(masks, part, first=False):
         for mask in masks:
-            target = flip(gz, mask)
-            interior = (target > 0) & (target < 7)
-
-            @pl.when(interior if inner else jnp.logical_not(interior))
-            def _():
-                piece_copy(mask, part).start()
-
-    FAR, NEAR = ((6, 7, 4, 5), (2, 3, 1, 0))
-    far_start, near_start = ((1 - half) * 48, half * 48)
+            either(
+                inner(flip(gz, mask)), lambda edge: piece_copy(mask, part, edge, first).start()
+            )
 
     def level_copy(kind, part, origin, target, mine=False):
-        every = kind < 3
+        every = kind < 3 or part == 3
         first = 0 if every else pl.multiple_of((origin // 4) * 24, 8)
         rows = pl.ds(first, 48 if every else 24)
         parts = pl.ds(part * 4, 4)
@@ -229,19 +335,52 @@
 
     mate, beside, across, past = (flip(gz, 1), flip(gz, 2), flip(gz, 6), flip(gz, 4))
 
-    for part in ORDER:
+    for copy in firsts + seconds:
+        copy.wait()
+    edges = (jnp.zeros((96, 128), F32), jnp.zeros((96, 128), F32))
+    edges = lax.fori_loop(0, 32, pack_edges, edges)
+    edge_out[0] = edges[0]
+    edge_out[1] = edges[1]
+    for copy in z_halos:
+        copy.start()
+    for masks, start in (((4, 5), 24 * ((gz // 2 + 2) % 4)), ((6, 7), 24 * (3 - gz // 2))):
+        make_rows(1, start, 24, False)
+        send_pieces(masks, 1, True)
+    for copy in thirds_in:
+        copy.wait()
+    for copy in x_halos:
+        copy.start()
+    for copy in z_halos:
+        copy.wait_recv()
+
+    for part in (2, 1, 0, 3):
+        if part == 1:
+            make_rows(part, far_start, 48)
+            send_patches()
         if part == 0:
+            for side in (0, 1):
+
+                @pl.when(jnp.logical_not(opens[side]))
+                def _():
+                    y_halos[1 - side].wait_recv()
+                    y_halos[side].start()
+
             for copy in x_halos:
                 copy.wait_recv()
-        make_rows(part, far_start, 48)
-        if part != 3:
-            send_pieces(FAR, part, True)
+        if part != 1:
+            make_rows(part, far_start, 48)
+            if part != 3:
+                send_pieces(FAR, part)
         make_rows(part, near_start, 48)
         if part != 3:
-            send_pieces(NEAR, part, True)
-
-    for copy in y_halos:
-        copy.wait_recv()
+            send_pieces(NEAR, part)
+
+    for side in (0, 1):
+
+        @pl.when(opens[side])
+        def _():
+            y_halos[1 - side].wait_recv()
+
 
     def fill_rows(x, carry):
         for spot, comp in enumerate((U, W)):
@@ -253,30 +392,40 @@
 
     lax.fori_loop(0, 32, fill_rows, 0)
     for part in ORDER:
-        make_rows(part, 0, 8)
-        make_rows(part, 88, 8)
-        for j in range(part * 4, part * 4 + 4):
-            halves[...] = lane_pairs(planes[2 * j] + planes[2 * j + 1], pair)
-            even = halves[pl.ds(0, 48, stride=2), :]
-            odd = halves[pl.ds(1, 48, stride=2), :]
-            own[j] = (even + odd) * 0.125
+        make_rows(part, 0, 8, side=0)
+        make_rows(part, 88, 8, side=1)
+        summed = [planes[2 * j] + planes[2 * j + 1] for j in range(part * 4, part * 4 + 4)]
+        halves[...] = lane_pairs_split(jnp.concatenate(summed, axis=0), pair)
+        for j in range(4):
+            even = halves[pl.ds(j * 96, 48, stride=2), :]
+            odd = halves[pl.ds(j * 96 + 1, 48, stride=2), :]
+            own[part * 4 + j] = (even + odd) * 0.125
         level_copy(3, part, gz, across, True).start()
         level_copy(1, part, gz, beside, True).start()
         level_copy(0, part, gz, mate, True).start()
         own_copy(part).start()
-    for part in ORDER:
-        send_pieces(FAR + NEAR, part, False)
-        if part == 3:
-            send_pieces(FAR + NEAR, part, True)
+    for mask in FAR + NEAR:
+
+        @pl.when(jnp.logical_not(inner(flip(gz, mask))))
+        def _():
+            row_copy(mask).start()
+
+    send_pieces(FAR[:2] + NEAR, 3)
 
     def pass_far(part):
         for mask in FAR:
-            piece_copy(mask, part).wait_recv()
+            piece_arrives(mask, part)
+        if part == 1:
+            apply_patches()
+            rows_arrive(FAR)
         parts = pl.ds(part * 8, 8)
+        rows = []
         for s in range(4):
             lanes = pl.ds(pl.multiple_of((1 - half) * 1024 + s * 256, 256), 256)
-            rows = [pencil[2 * r, parts, lanes] + pencil[2 * r + 1, parts, lanes] for r in range(6)]
-            thirds[s] = lane_pairs(jnp.concatenate(rows, axis=0), pair)
+            rows += [pencil[2 * r, parts, lanes] + pencil[2 * r + 1, parts, lanes] for r in range(6)]
+        pooled = lane_pairs_split(jnp.concatenate(rows, axis=0), pair)
+        for s in range(4):
+            thirds[s] = pooled[s * 48 : s * 48 + 48]
             for j in range(4):
                 even = thirds[s, pl.ds(2 * j, 6, stride=8), :]
                 odd = thirds[s, pl.ds(2 * j + 1, 6, stride=8), :]
@@ -292,8 +441,10 @@
     for part in ORDER:
         level_copy(1, part, beside, beside).wait_recv()
         level_copy(2, part, beside, mate).start()
-    for part in ORDER[:3]:
-        pass_far(part)
+    pass_far(1)
+    send_pieces(FAR[2:], 3)
+    pass_far(2)
+    pass_far(0)
     for part in ORDER:
         pass_level(part)
     for part in ORDER[:3]:
@@ -302,23 +453,16 @@
     for part in ORDER:
         level_copy(4, part, past, beside).wait_recv()
         level_copy(6, part, past, mate).start()
-    pass_far(3)
-    far_copy(8, 3, beside, beside).wait_recv()
-    far_copy(9, 3, beside, mate).start()
 
     for part in ORDER:
         own_copy(part).wait()
-        piece_copy(0, part).wait()
-        for mask in range(1, 8):
-            piece_copy(mask, part).wait_send()
-        for mask in (1, 2, 3):
-            piece_copy(mask, part).wait_recv()
         level_copy(0, part, mate, mate).wait_recv()
         level_copy(2, part, flip(gz, 3), mate).wait_recv()
         level_copy(5, part, flip(gz, 7), mate).wait_recv()
         level_copy(6, part, flip(gz, 5), mate).wait_recv()
-        far_copy(7, part, mate, mate).wait_recv()
-        far_copy(9, part, flip(gz, 3), mate).wait_recv()
+        if part != 3:
+            far_copy(7, part, mate, mate).wait_recv()
+            far_copy(9, part, flip(gz, 3), mate).wait_recv()
 
     for side in (0, 1):
 
@@ -332,7 +476,7 @@
                     level[j, rows, lanes] = far[d, j, 0:6, :]
                     return carry
 
-                lax.fori_loop(0, 16, place_rows, 0)
+                lax.fori_loop(0, 12, place_rows, 0)
 
     for part in ORDER:
         level_copy(0, part, gz, mate).wait_send()
@@ -342,11 +486,32 @@
         level_copy(4, part, across, beside).wait_send()
         level_copy(5, part, across, mate).wait_send()
         level_copy(6, part, past, mate).wait_send()
-        far_copy(7, part, gz, mate).wait_send()
-        far_copy(8, part, gz, beside).wait_send()
-        far_copy(9, part, beside, mate).wait_send()
+        if part != 3:
+            far_copy(7, part, gz, mate).wait_send()
+            far_copy(8, part, gz, beside).wait_send()
+            far_copy(9, part, beside, mate).wait_send()
     for copy in z_halos + y_halos + x_halos:
         copy.wait_send()
+    for mask in FAR:
+        patch_copy(mask).wait_send()
+    for mask in range(1, 8):
+
+        @pl.when(jnp.logical_not(inner(flip(gz, mask))))
+        def _():
+            row_copy(mask).wait_send()
+
+    rows_arrive((1, 2, 3))
+
+    @pl.when(jnp.logical_not(inside))
+    def _():
+        row_copy(0).wait()
+
+    for part in ORDER:
+        either(inside, lambda edge: piece_copy(0, part, edge).wait())
+        for mask in range(1, 8):
+            either(inner(flip(gz, mask)), lambda edge: piece_copy(mask, part, edge).wait_send())
+        for mask in (1, 2, 3) + (FAR if part == 3 else ()):
+            piece_arrives(mask, part)
 
 
 def finish(
@@ -354,8 +519,11 @@
     two_half, three_half, four_half, five_half, three_at, four_at, sems,
 ):
     copies = [
-        pltpu.make_async_copy(pencil, mag_out, sems.at[0]),
-        pltpu.make_async_copy(level, one_out, sems.at[1]),
+        pltpu.make_async_copy(pencil.at[i * 3 : i * 3 + 3], mag_out.at[i * 3 : i * 3 + 3], sems.at[0, i])
+        for i in range(4)
+    ] + [
+        pltpu.make_async_copy(level.at[i * 4 : i * 4 + 4], one_out.at[i * 4 : i * 4 + 4], sems.at[1, i])
+        for i in range(4)
     ]
     for copy in copies:
         copy.start()
@@ -419,14 +587,20 @@
             vmem((32, 96, 256), F32),
             vmem((96, 32, 256), F32),
             vmem((16, 48, 128), F32),
-            vmem((96, 128), F32),
+            vmem((384, 128), F32),
             vmem((4, 48, 128), F32),
             vmem((2, 96, 128), F32),
             vmem((2, 96, 128), F32),
             vmem((2, 2, 32, 2, 128), F32),
             vmem((2, 2, 32, 2, 128), F32),
-            vmem((4, 16, 8, 512), F32),
-            dma((3, 4)),
+            vmem((4, 12, 8, 512), F32),
+            vmem((48, 8, 256), F32),
+            vmem((4, 8, 128), F32),
+            vmem((4, 8, 128), F32),
+            vmem((2, 32, 256), F32),
+            dma((2, 4)),
+            dma((2, 8)),
+            dma((4, 4)),
             dma((2, 2)),
             dma((2, 2)),
             dma((2, 2)),
@@ -434,7 +608,7 @@
             dma((8, 4)),
             dma((10, 4)),
             dma((8, 4)),
-            dma((4, 4)),
+            dma((4, 3)),
             dma((2, 4)),
         ],
         compiler_params=pltpu.CompilerParams(
@@ -463,7 +637,7 @@
             vmem((6, 128), F32),
             vmem((4, 12, 256), F32),
             vmem((2, 6, 128), F32),
-            dma((2,)),
+            dma((2, 4)),
         ],
         compiler_params=pltpu.CompilerParams(vmem_limit_bytes=16 * 1024 * 1024),
     )(pltpu.with_memory_space_constraint(pencil, vmem), pltpu.with_memory_space_constraint(level, vmem))

time: 103 us -> 103 us (level)
  no operation moved by 1% of the time
where the time goes in v3:
time: 103 us; the launch traced here: 101 us
  Pallas kernels  100 us (97%)
    pallas_call x1, Pallas kernels, on_device(): pl.pallas_call(exchange, name='exchange', out_shape=(vmem((12, 32, 2048),...  96.8 us
    pallas_call x1, Pallas kernels, on_device(): pl.pallas_call(finish, name='finish', out_shape=(jax.ShapeDtypeStruct((12...  3.61 us

profile of v3, /device:TPU:2, one launch (start us, length us, event | category | flops | bytes accessed | tf_op | source)
XLA Modules:
  0.0 101.0 jit_solution(4698086444444849445)
XLA Ops:
  0.6 96.8 %exchange.1 = (f32[12,32,2048]{2,1,0:T(8,128)S(1)}, f32[16,48,1024]{2,1,0:T(8,128)S(1)}) custom-call(f32[3,32,96,256]{3,2,1,0:T(8,128)} %vel_hbm.1), custom_call_target="tpu_custom_call" | custom-call | tf_op jit(solution)/shard_map/exchange/pallas_call | solution.py:579
  97.4 3.6 %finish.1 = (f32[12,32,2048]{2,1,0:T(8,128)}, f32[16,48,1024]{2,1,0:T(8,128)}, f32[8,24,512]{2,1,0:T(8,128)}, f32[12,4,256]{2,1,0:T(4,128)}, f32[6,2,128]{2,1,0:T(2,128)}, /*index=5*/f32[3,1,64]{2,1,0:T(1,128)}) custom-call(f32[12,32,2048]{2,1,0:T(8,128)S(1)} %get-tuple-element.14.pencil, f32[16,48,1024]{2,1,0:T(8,128)S(1)} %get-tuple-element.15.level), custom_call_target="tpu_custom_call" | custom-call | tf_op jit(solution)/shard_map/finish/pallas_call | solution.py:620

commit v4 on v3

--- a/solution.py
+++ b/solution.py
@@ -400,9 +400,9 @@
             even = halves[pl.ds(j * 96, 48, stride=2), :]
             odd = halves[pl.ds(j * 96 + 1, 48, stride=2), :]
             own[part * 4 + j] = (even + odd) * 0.125
-        level_copy(3, part, gz, across, True).start()
         level_copy(1, part, gz, beside, True).start()
         level_copy(0, part, gz, mate, True).start()
+        level_copy(3, part, gz, across, True).start()
         own_copy(part).start()
     for mask in FAR + NEAR:
 

time: 103 us -> 103 us (level)
  no operation moved by 1% of the time
where the time goes in v4:
time: 103 us; the launch traced here: 101 us
  Pallas kernels  100 us (97%)
    pallas_call x1, Pallas kernels, on_device(): pl.pallas_call(exchange, name='exchange', out_shape=(vmem((12, 32, 2048),...  96.8 us
    pallas_call x1, Pallas kernels, on_device(): pl.pallas_call(finish, name='finish', out_shape=(jax.ShapeDtypeStruct((12...  3.61 us

profile of v4, /device:TPU:2, one launch (start us, length us, event | category | flops | bytes accessed | tf_op | source)
XLA Modules:
  0.0 101.0 jit_solution(15758843664436123571)
XLA Ops:
  0.6 96.8 %exchange.1 = (f32[12,32,2048]{2,1,0:T(8,128)S(1)}, f32[16,48,1024]{2,1,0:T(8,128)S(1)}) custom-call(f32[3,32,96,256]{3,2,1,0:T(8,128)} %vel_hbm.1), custom_call_target="tpu_custom_call" | custom-call | tf_op jit(solution)/shard_map/exchange/pallas_call | solution.py:579
  97.4 3.6 %finish.1 = (f32[12,32,2048]{2,1,0:T(8,128)}, f32[16,48,1024]{2,1,0:T(8,128)}, f32[8,24,512]{2,1,0:T(8,128)}, f32[12,4,256]{2,1,0:T(4,128)}, f32[6,2,128]{2,1,0:T(2,128)}, /*index=5*/f32[3,1,64]{2,1,0:T(1,128)}) custom-call(f32[12,32,2048]{2,1,0:T(8,128)S(1)} %get-tuple-element.14.pencil, f32[16,48,1024]{2,1,0:T(8,128)S(1)} %get-tuple-element.15.level), custom_call_target="tpu_custom_call" | custom-call | tf_op jit(solution)/shard_map/finish/pallas_call | solution.py:620
